TPU v7x, 32 devices: a whole 2x2x4 slice. The times are simulated.
32 devices in a mesh: dp: 4 (over y, core), head: 2 (over x), kv: 4 (over z).
Axes of the slice: x: 2, y: 2, z: 4, core: 2. Of those that a mesh axis runs over, the one named last changes fastest.
Arguments:
- teacher_query: bfloat16 [4, 1024, 3584], P('dp', 'kv', 'head'), may hold values from -96 to 96
- teacher_key: bfloat16 [4, 1024, 512], P('dp', 'kv', 'head'), may hold values from -8 to 8
- student_query: bfloat16 [4, 1024, 1792], P('dp', 'kv', 'head'), may hold values from -96 to 96
- student_key: bfloat16 [4, 1024, 256], P('dp', 'kv', 'head'), may hold values from -8 to 8
- pair_table: int32 [14, 2], replicated, may hold values from 0 to 27, as said below
Outputs:
- kl: float32 [4, 14, 1024], P('dp', 'head', 'kv')
- head_loss: float32 [14], P('head')
Inputs may be any that keep to these rules, and one draw needn't show every extreme that they name: `pair_table`: each of the 28 teacher heads appears exactly once in the table.
All inputs are finite; a program needn't handle non-finite values.
Results may differ from a plain program's by a relative error of at most 0.0003.
Values may be sent and summed in bfloat16 or wider, within the bound.
A program may use at most 64 MiB of HBM per device.

v0:
```python
import math

import jax
import jax.numpy as jnp
from jax import lax
from jax.sharding import PartitionSpec as P

HT = 28
KVT = 4
DH = 128
HS = 14
KVS = 2


masked_value = -1e30


def running_softmax(running_max, running_total, logits, causal_mask):
    filled = jnp.where(causal_mask, logits, masked_value)
    new_max = jnp.maximum(running_max, jnp.max(filled, axis=-1))
    rescale = jnp.exp(running_max - new_max)
    weights = jnp.where(causal_mask, jnp.exp(filled - new_max[..., None]), 0.0)
    return (new_max, running_total * rescale + jnp.sum(weights, axis=-1), rescale, weights)


def make_fold(teacher_heads, teacher_select, student_heads, student_select, repeat, query_pos):
    seq_dev, row_count, pair_count, head_dim = teacher_heads.shape
    student_count = student_heads.shape[2]
    scale = 1.0 / math.sqrt(head_dim)
    last_query = query_pos[row_count - 1]

    def fold_step(carry, pieces, start):
        teacher_keys, student_keys = pieces
        key_count = teacher_keys.shape[1]
        block_size = math.gcd(key_count, 512)
        block_total = key_count // block_size
        visible = jnp.clip(last_query // block_size + 1, 0, block_total)

        def one_block(block_index, state):
            t_max, t_total, t_cross, s_max, s_total = state
            offset = block_index * block_size
            t_block = lax.dynamic_slice_in_dim(teacher_keys, offset, block_size, 1).reshape(
                seq_dev, block_size, -1, head_dim
            )
            s_block = lax.dynamic_slice_in_dim(student_keys, offset, block_size, 1).reshape(
                seq_dev, block_size, -1, head_dim
            )
            t_keys = jnp.take(t_block, teacher_select, axis=2)
            s_keys = jnp.take(s_block, student_select, axis=2)
            t_logits = (
                jnp.einsum(
                    "bqpd,bkpd->bpqk", teacher_heads, t_keys, preferred_element_type=jnp.float32
                )
                * scale
            )
            s_logits = (
                jnp.einsum(
                    "bqsd,bksd->bsqk", student_heads, s_keys, preferred_element_type=jnp.float32
                )
                * scale
            )
            key_pos = offset + jnp.arange(block_size, dtype=jnp.int32)
            causal_mask = key_pos[None, :] <= query_pos[:, None]
            t_max, t_total, t_rescale, t_weights = running_softmax(
                t_max, t_total, t_logits, causal_mask
            )
            s_max, s_total, s_rescale, s_weights = running_softmax(
                s_max, s_total, s_logits, causal_mask
            )
            split_logits = t_logits.reshape(seq_dev, student_count, repeat, row_count, block_size)
            gap = (split_logits - s_logits[:, :, None]).reshape(
                seq_dev, pair_count, row_count, block_size
            )
            t_cross = t_cross * t_rescale + jnp.sum(t_weights * gap, axis=-1)
            return (t_max, t_total, t_cross, s_max, s_total)

        return lax.fori_loop(0, visible, one_block, carry)

    pair_shape = (seq_dev, pair_count, row_count)
    student_shape = (seq_dev, student_count, row_count)
    initial = (
        jnp.full(pair_shape, masked_value, jnp.float32),
        jnp.zeros(pair_shape, jnp.float32),
        jnp.zeros(pair_shape, jnp.float32),
        jnp.full(student_shape, masked_value, jnp.float32),
        jnp.zeros(student_shape, jnp.float32),
    )
    return (fold_step, initial)


def finish_pairs(state, repeat):
    t_max, t_total, t_cross, s_max, s_total = state
    seq_dev, pair_count, row_count = t_max.shape
    student_count = s_max.shape[1]
    t_lse = t_max + jnp.log(t_total)
    s_lse = s_max + jnp.log(s_total)
    s_paired = jnp.broadcast_to(
        s_lse[:, :, None], (seq_dev, student_count, repeat, row_count)
    ).reshape(seq_dev, pair_count, row_count)
    return t_cross / t_total - t_lse + s_paired


def per_device(teacher_query, teacher_key, student_query, student_key, pair_table):
    seq_dev, row_count, teacher_width = teacher_query.shape
    n_head = lax.axis_size("head")
    n_kv = lax.axis_size("kv")
    n_data = lax.axis_size("dp")
    head_index = lax.axis_index("head")
    kv_index = lax.axis_index("kv")
    group_teacher = HT // KVT
    group_student = HS // KVS
    local_student = HS // n_head
    local_student_kv = KVS // n_head
    query_pos = kv_index * row_count + jnp.arange(row_count, dtype=jnp.int32)
    all_tq, all_tk = (
        lax.all_gather(teacher_query, "head", axis=2, tiled=True),
        lax.all_gather(teacher_key, "head", axis=2, tiled=True),
    )
    my_pairs = lax.dynamic_slice_in_dim(
        pair_table, head_index * local_student, local_student, 0
    ).reshape(-1)
    teacher_heads = jnp.take(all_tq.reshape(seq_dev, row_count, HT, DH), my_pairs, axis=2)
    teacher_select = my_pairs // group_teacher
    student_heads = student_query.reshape(seq_dev, row_count, local_student, DH)
    student_ids = head_index * local_student + jnp.arange(local_student, dtype=jnp.int32)
    student_select = student_ids // group_student - head_index * local_student_kv
    fold_step, initial = make_fold(
        teacher_heads, teacher_select, student_heads, student_select, 2, query_pos
    )
    state = fold_step(
        initial,
        (
            lax.all_gather(all_tk, "kv", axis=1, tiled=True),
            lax.all_gather(student_key, "kv", axis=1, tiled=True),
        ),
        jnp.int32(0),
    )
    pair_kl = finish_pairs(state, 2)
    kl_local = jnp.sum(pair_kl.reshape(seq_dev, local_student, 2, row_count), axis=2)
    head_sums = jnp.sum(kl_local, axis=(0, 2))
    total = lax.psum(head_sums, ("dp", "kv"))
    head_loss = total / (seq_dev * n_data * row_count * n_kv)
    return (kl_local, head_loss)


def solution(mesh):
    in_specs = (
        P("dp", "kv", "head"),
        P("dp", "kv", "head"),
        P("dp", "kv", "head"),
        P("dp", "kv", "head"),
        P(),
    )
    out_specs = (P("dp", "head", "kv"), P("head"))
    return jax.shard_map(
        per_device, mesh=mesh, in_specs=in_specs, out_specs=out_specs, check_vma=False
    )
```

profile of v0, /device:TPU:0, one launch (start us, length us, event | category | flops | bytes accessed | tf_op | source)
XLA Modules:
  0.0 131.6 jit_solution(168695083922571773)
XLA Ops:
  7.2 0.0 copy-start
  7.2 0.0 copy-start.1
  7.2 0.0 copy-start.2
  7.2 0.0 all-gather.5.cloned.1.call-start
  7.2 2.3 %copy.18 = bf16[1,256,1792]{1,2,0:T(8,128)(2,1)} copy(bf16[1,256,1792]{2,1,0:T(8,128)(2,1)} %param.7) | data formatting | bytes 1835008 | tf_op args[0]
  9.5 0.0 all-gather.5.cloned.1.call-update
  9.5 0.0 all-gather.3.cloned.1.call-start
  9.6 1.0 copy.17
  10.6 7.2 %all_gather.12 = bf16[1,256,512]{1,2,0:T(8,128)(2,1)} all-gather(bf16[1,256,256]{1,2,0:T(8,128)(2,1)S(1)} %copy.17), channel_id=1, replica_groups=mesh['dp'=4,'head'=2,'kv'=4] {'head'}, dimensions={2}, use_global_device_ids=true | all-gather | bytes 393216 | tf_op jit(solution)/shard_map/all_gather | solution.py:117
  17.8 0.0 all-gather.3.cloned.1.call-update
  17.9 0.6 slice.3
  20.1 0.0 copy-done
  20.1 0.1 constant_dynamic-slice_fusion.1
  20.2 0.1 copy.16
  20.2 0.1 reshape.172
  20.3 0.1 reshape.174
  21.0 0.0 copy-done.1
  21.0 0.2 copy.21
  21.2 0.3 copy.22
  21.5 0.0 copy-done.2
  21.5 14.4 %all_gather.15 = bf16[1,1024,128]{2,1,0:T(8,128)(2,1)S(1)} all-gather(bf16[1,256,128]{2,1,0:T(8,128)(2,1)S(1)} %copy-done.2), channel_id=1, replica_groups=mesh['dp'=4,'head'=2,'kv'=4] {'kv'}, dimensions={1}, use_global_device_ids=true | all-gather | bytes 327680 | tf_op jit(solution)/shard_map/all_gather | solution.py:134
  35.9 6.6 %all-gather.5.cloned.1.call-done = bf16[1,256,3584]{1,2,0:T(8,128)(2,1)} async-done(((bf16[1,256,1792]{1,2,0:T(8,128)(2,1)}), bf16[1,256,3584]{1,2,0:T(8,128)(2,1)}) %all-gather.5.cloned.1.call-update) | async-done | bytes 1835024 | tf_op jit(solution)/shard_map/all_gather | solution.py:116
  42.5 2.9 %copy.20 = bf16[256,28,128]{2,0,1:T(8,128)(2,1)S(1)} copy(bf16[256,28,128]{0,2,1:T(8,128)(2,1)} %bitcast.99) | data formatting | bytes 3670016 | tf_op jit(solution)/shard_map/reshape | solution.py:122
  45.4 0.7 gather_fusion.1
  46.2 1.1 bitcast_select_fusion.1
  47.3 26.8 %all-gather.3.cloned.1.call-done = bf16[1,1024,512]{1,2,0:T(8,128)(2,1)} async-done(((bf16[1,256,512]{1,2,0:T(8,128)(2,1)}), bf16[1,1024,512]{1,2,0:T(8,128)(2,1)}) %all-gather.3.cloned.1.call-update) | async-done | bytes 1048592 | tf_op jit(solution)/shard_map/all_gather | solution.py:133
  74.1 9.4 %while.19 = (s32[]{:T(128)}, f32[1,14,256]{2,1,0:T(8,128)S(1)}, f32[1,14,256]{2,1,0:T(8,128)S(1)}, f32[1,14,256]{2,1,0:T(8,128)S(1)}, f32[1,7,256]{2,1,0:T(8,128...) while((s32[]{:T(128)}, f32[1,14,256]{2,1,0:T(8,128)S(1)}, ...), condition=%wide.region_6.7_spmd.clone, body=%wide.region_0.6_spmd.clone.sunk | while | flops 732774400 | bytes 36064820 | solution.py:77
  74.1 1.1 constant_dynamic-slice_fusion.3
  75.2 0.3 copy.24
  75.5 0.9 gather_fusion
  76.4 0.1 broadcast_compare_fusion.2
  76.6 2.6 %fusion.28 = (f32[14,256]{1,0:T(8,128)S(1)}, f32[14,512,256]{2,1,0:T(8,128)S(1)}) fusion(pred[256,512]{0,1:T(8,128)(4,1)S(1)} %broadcast_compare_fusion.2, bf16[1,256,14,128]{3,1,2,0:T(8,128)(2,1)} %get-tuple-element.346, bf16[14,512,128]{2,1,0:T(8,128)(2,1)S(1)} %gather_fusion, pred[14]{0:T(512)(128)(4,1)S(1)} %compare_and_fusion.5), kind=kOutput, calls=%fused_computation.9.clone.1 | convolution fusion | flops 476180992 | bytes 10237966 | tf_op jit(solution)/shard_map/while/body/bqpd,bkpd->bpqk/dot_general | solution.py:51
  79.3 0.8 select_reduce_fusion.4
  80.1 2.6 %fusion.29 = (f32[14,256]{1,0:T(8,128)S(1)}, f32[14,256]{1,0:T(8,128)S(1)}) fusion(f32[14,512,256]{2,1,0:T(8,128)S(1)} %get-tuple-element.292, f32[7,256,512]{1,2,0:T(8,128)S(1)} %get-tuple-element.293, f32[14,256]{1,0:T(8,128)S(1)} %bitcast.97, pred[256,512]{0,1:T(8,128)(4,1)S(1)} %broadcast_compare_fusion.2), kind=kLoop, calls=%fused_computation.6.clone.1 | loop fusion | flops 14672896 | bytes 11184128 | tf_op jit(solution)/shard_map/while/body/reduce_sum | solution.py:74
  82.7 0.8 select_reduce_fusion.5
  83.6 0.1 fusion.23
  83.7 0.1 reduce_sum.63
  83.8 0.1 reduce_sum.64
  83.9 0.6 reduce_sum.61
  84.5 39.7 %psum.7 = f32[7]{0:T(128)S(1)} all-reduce(f32[7]{0:T(128)S(1)} %reduce_sum.64), channel_id=1, replica_groups=mesh['dp'=4,'head'=2,'kv'=4] {'dp','kv'}, use_global_device_ids=true, to_apply=%region_10.11 | all-reduce | flops 7 | bytes 56 | tf_op jit(solution)/shard_map/psum | solution.py:141
  124.3 0.5 broadcast_multiply_fusion
  (28 shorter events, 0.2 us)
Async XLA Ops:
  7.2 12.9 %copy-start = (s32[14,2]{0,1:T(2,128)S(1)}, s32[14,2]{0,1:T(2,128)}, u32[]{:S(2)}) copy-start(s32[14,2]{0,1:T(2,128)} %param.11) | copy-start | bytes 340
  7.2 13.8 %copy-start.1 = (bf16[1,256,896]{2,1,0:T(8,128)(2,1)S(1)}, bf16[1,256,896]{2,1,0:T(8,128)(2,1)}, u32[]{:S(2)}) copy-start(bf16[1,256,896]{2,1,0:T(8,128)(2,1)} %param.9) | copy-start | bytes 1376260
  7.2 14.3 %copy-start.2 = (bf16[1,256,128]{2,1,0:T(8,128)(2,1)S(1)}, bf16[1,256,128]{2,1,0:T(8,128)(2,1)}, u32[]{:S(2)}) copy-start(bf16[1,256,128]{2,1,0:T(8,128)(2,1)} %param.10) | copy-start | bytes 196612
  7.2 35.3 %all-gather.5.cloned.1.call-start = ((), (), s32[]{:S(2)}) async-start(), calls=%async_computation.1 | async-start | bytes 2752512 | tf_op jit(solution)/shard_map/all_gather | solution.py:116
  9.5 64.5 %all-gather.3.cloned.1.call-start = ((), (), s32[]{:S(2)}) async-start(), calls=%async_computation | async-start | bytes 1310720 | tf_op jit(solution)/shard_map/all_gather | solution.py:133
Sparse Core Ops, SparseCore 0:
  9.7 32.8 all-gather.4
  44.1 29.9 all-gather.2
where the time goes:
time: 132 us
  blocking collectives  61.4 us (47%)
  waiting for transfers between devices  33.5 us (25%)
  between operations  16.4 us (12%)
  local copies, waits for them, and re-layouts  11.3 us (9%)
  other arithmetic  5.49 us (4%)
  matrix products  3.37 us (3%)
    psum x1, blocking collectives, per_device(): total = lax.psum(head_sums, ('dp', 'kv'))  39.7 us
    all_gather x1, waiting for transfers between devices, per_device(): lax.all_gather(all_tk, 'kv', axis=1, tiled=True)  26.8 us
    all_gather x1, blocking collectives, per_device(): lax.all_gather(student_key, 'kv', axis=1, tiled=True)  14.4 us
    all_gather x1, blocking collectives, per_device(): lax.all_gather(teacher_key, 'head', axis=2, tiled=True)  7.22 us
    all_gather x1, waiting for transfers between devices, per_device(): lax.all_gather(teacher_query, 'head', axis=2, tiled=True)  6.6 us
    unnamed x10, local copies, waits for them, and re-layouts  3.76 us
    reshape x1, local copies, waits for them, and re-layouts, per_device(): all_tq.reshape(seq_dev, row_count, HT, DH)  2.89 us
  transfers between devices with their start and end apart: 2, of which 2 were waited for; matrix products, arithmetic and copies ran while one was open for 5% of the time, Pallas kernels for 0%

commit v1 on v0

v1 whole, which is shorter than its diff:
```python
import functools
import math

import jax
import jax.numpy as jnp
from jax import lax
from jax.experimental import pallas as pl
from jax.experimental.pallas import tpu as pltpu
from jax.sharding import PartitionSpec as P

HT = 28
KVT = 4
DH = 128
HS = 14
KVS = 2

MESH = pl.DeviceIdType.MESH
LOWEST = -1e30


def nn(a, b):
    return jnp.dot(a, b, preferred_element_type=jnp.float32)


def flip(x):
    n = x.shape[1]
    eye = (
        lax.broadcasted_iota(jnp.int32, (n, n), 0) == lax.broadcasted_iota(jnp.int32, (n, n), 1)
    ).astype(jnp.bfloat16)
    out = lax.dot_general(eye, x, (((1,), (1,)), ((), ())), preferred_element_type=jnp.float32)
    return out.astype(jnp.bfloat16)


def kernel(
    n_dp, n_head, n_kv, rows,
    table, tq_hbm, tk_hbm, sq_hbm, sk_hbm,
    kl_ref, loss_ref,
    tq, tk, sq, sk,
    tq_t, sq_t, key_t, mixed, t_max, s_max, s_sum,
    inverse, acc, acc_in, sums,
    load_sem, x_send, x_recv, z_send, z_recv, sum_send, sum_recv,
):
    n_t, n_s = HT // n_head, HS // n_head
    g_t, g_s = KVT // n_head, KVS // n_head
    per_t, per_s = HT // KVT, HS // KVS
    dp, hd, kv = lax.axis_index("dp"), lax.axis_index("head"), lax.axis_index("kv")
    n_rank = n_dp * n_kv
    rank = dp * n_kv + kv
    scale = 1.0 / math.sqrt(DH)
    rate = scale * math.log2(math.e)

    loads = [
        pltpu.make_async_copy(sk_hbm.at[0], sk.at[hd, kv], load_sem.at[0]),
        pltpu.make_async_copy(tk_hbm.at[0], tk.at[kv], load_sem.at[1]),
        pltpu.make_async_copy(sq_hbm.at[0], sq.at[hd], load_sem.at[2]),
        pltpu.make_async_copy(tq_hbm.at[0], tq, load_sem.at[3]),
    ]
    for load in loads:
        load.start()

    barrier = pltpu.get_barrier_semaphore()

    def greet(peer, carry):
        @pl.when(peer != rank)
        def _():
            pl.semaphore_signal(
                barrier, inc=1, device_id={"dp": peer // n_kv, "kv": peer % n_kv},
                device_id_type=MESH,
            )
        return carry

    for step in range(1, n_head):
        pl.semaphore_signal(
            barrier, inc=1, device_id={"head": (hd + step) % n_head}, device_id_type=MESH
        )
    lax.fori_loop(0, n_rank, greet, 0)

    entries = [table[k // 2, k % 2] for k in range(HT)]
    for t in range(n_t):
        found = jnp.int32(0)
        for k in range(HT):
            found = jnp.where(entries[k] == hd * n_t + t, k // 2, found)
        inverse[t] = found

    for load in loads:
        load.wait()
    pl.semaphore_wait(barrier, n_rank - 1 + n_head - 1)

    def across(slot, step, src, dst):
        return pltpu.make_async_remote_copy(
            src_ref=src, dst_ref=dst, send_sem=x_send.at[slot, step - 1],
            recv_sem=x_recv.at[slot, step - 1],
            device_id={"head": (hd + step) % n_head}, device_id_type=MESH,
        )

    def upward(block, piece):
        ref = tk.at[block] if piece is n_head else sk.at[piece, block]
        return pltpu.make_async_remote_copy(
            src_ref=ref, dst_ref=ref, send_sem=z_send.at[block, piece],
            recv_sem=z_recv.at[block, piece],
            device_id={"kv": jnp.minimum(kv + 1, n_kv - 1)}, device_id_type=MESH,
        )

    pieces = [n_head] + [(hd + s) % n_head for s in range(n_head)]
    not_last = kv < n_kv - 1

    keys_over = [across(0, s, sk.at[hd, kv], sk.at[hd, kv]) for s in range(1, n_head)]
    queries_over = [across(1, s, sq.at[hd], sq.at[hd]) for s in range(1, n_head)]
    for copy in keys_over:
        copy.start()

    @pl.when(not_last)
    def _():
        upward(kv, n_head).start()
        upward(kv, hd).start()

    for copy in queries_over:
        copy.start()

    for h in range(n_t):
        tq_t[h] = flip(tq[:, h * DH:(h + 1) * DH])
    for h in range(n_s):
        sq_t[hd * n_s + h] = flip(sq[hd, :, h * DH:(h + 1) * DH])

    key_t[:, 2 * DH:] = jnp.ones((g_t * KVS, 16, rows), jnp.bfloat16)
    for copy in keys_over:
        copy.wait()

    @pl.when(not_last)
    def _():
        for s in range(1, n_head):
            upward(kv, (hd + s) % n_head).start()

    visible = lax.broadcasted_iota(jnp.int32, (rows, rows), 0) <= lax.broadcasted_iota(
        jnp.int32, (rows, rows), 1
    )

    def fold(block, diagonal):
        for g in range(g_t):
            flipped = flip(tk[block, :, g * DH:(g + 1) * DH])
            for j in range(KVS):
                key_t[g * KVS + j, :DH] = flipped
        for j in range(KVS):
            flipped = flip(sk[j // g_s, block, :, j % g_s * DH:(j % g_s + 1) * DH])
            for g in range(g_t):
                key_t[g * KVS + j, DH:2 * DH] = flipped

        def weigh(logits, high, row):
            if diagonal:
                logits = jnp.where(visible, logits, LOWEST)
            top = jnp.max(logits, axis=0, keepdims=True)
            if diagonal:
                decay = None
            else:
                old = high[row]
                top = jnp.maximum(old, top)
                decay = jnp.exp2((old - top) * rate)
            weights = jnp.exp2((logits - top) * rate)
            high[row] = top
            return weights, decay

        for h in range(n_t):
            g = h // per_t
            logits = nn(tk[block, :, g * DH:(g + 1) * DH], tq_t[h])
            weights, decay = weigh(logits, t_max, h)
            part = nn(key_t[g * KVS + inverse[h] // per_s], weights.astype(jnp.bfloat16))
            mixed[h] = part if diagonal else mixed[h] * decay + part
        for h in range(n_s):
            g = h // per_s
            logits = nn(sk[hd, block, :, g * DH:(g + 1) * DH], sq_t[hd * n_s + h])
            weights, decay = weigh(logits, s_max, h)
            part = jnp.sum(weights, axis=0, keepdims=True)
            s_sum[h] = part if diagonal else s_sum[h] * decay + part

    fold(kv, True)

    def step(s, carry):
        block = kv - s
        for piece in pieces:
            upward(block, piece).wait_recv()

            @pl.when(not_last)
            def _():
                upward(block, piece).start()
        fold(block, False)
        return carry

    lax.fori_loop(1, kv + 1, step, 0)

    for copy in queries_over:
        copy.wait()
    for s in range(1, n_head):
        d = (hd + s) % n_head
        for h in range(n_s):
            sq_t[d * n_s + h] = flip(sq[d, :, h * DH:(h + 1) * DH])

    pad = acc.shape[0] // n_head
    place = lax.broadcasted_iota(jnp.int32, acc.shape, 0)
    total = jnp.zeros(acc.shape, jnp.float32)
    for h in range(n_t):
        partner = inverse[h]
        own = mixed[h, :DH] * tq_t[h].astype(jnp.float32)
        other = mixed[h, DH:2 * DH] * sq_t[partner].astype(jnp.float32)
        mass = mixed[h, 2 * DH:2 * DH + 1]
        value = jnp.sum(own - other, axis=0, keepdims=True) * scale / mass
        value = value - (t_max[h] * scale + jnp.log(mass))
        row = (partner // n_s) * pad + partner % n_s
        total = total + jnp.where(place == row, value, 0.0)
    acc[...] = total

    returns = [
        across(2, s, acc.at[pl.ds(((hd + s) % n_head) * pad, pad)], acc_in.at[s - 1])
        for s in range(1, n_head)
    ]
    for copy in returns:
        copy.start()
    lse = jnp.concatenate(
        [s_max[h] * scale + jnp.log(s_sum[h]) for h in range(n_s)]
        + [jnp.zeros((1, rows), jnp.float32)] * (pad - n_s),
        axis=0,
    )
    kl = acc[pl.ds(hd * pad, pad)] + 2.0 * lse
    for s in range(1, n_head):
        returns[s - 1].wait()
        kl = kl + acc_in[s - 1]
    kl_ref[0] = kl[:n_s]
    sums[rank] = jnp.broadcast_to(jnp.sum(kl, axis=1, keepdims=True), (pad, 128))

    def share(peer, place):
        return pltpu.make_async_remote_copy(
            src_ref=sums.at[rank], dst_ref=sums.at[rank],
            send_sem=sum_send.at[peer], recv_sem=sum_recv.at[place],
            device_id={"dp": peer // n_kv, "kv": peer % n_kv}, device_id_type=MESH,
        )

    def send(peer, carry):
        @pl.when(peer != rank)
        def _():
            share(peer, rank).start()
        return carry

    def land(peer, carry):
        @pl.when(peer != rank)
        def _():
            share(peer, rank).wait_send()
            share(peer, peer).wait_recv()
        return carry

    lax.fori_loop(0, n_rank, send, 0)

    @pl.when(not_last)
    def _():
        def drain(block, carry):
            for piece in pieces:
                upward(block, piece).wait_send()
            return carry
        lax.fori_loop(0, kv + 1, drain, 0)

    lax.fori_loop(0, n_rank, land, 0)
    whole = jnp.sum(sums[...], axis=0)
    diagonal = lax.broadcasted_iota(jnp.int32, whole.shape, 0) == lax.broadcasted_iota(
        jnp.int32, whole.shape, 1
    )
    line = jnp.sum(jnp.where(diagonal, whole, 0.0), axis=0, keepdims=True)
    loss_ref[...] = line[:, :n_s] / (n_dp * rows * n_kv)


def per_device(teacher_query, teacher_key, student_query, student_key, pair_table):
    n_dp, n_head, n_kv = lax.axis_size("dp"), lax.axis_size("head"), lax.axis_size("kv")
    seq_dev, rows, wide_t = teacher_query.shape
    assert seq_dev == 1
    n_t, n_s = HT // n_head, HS // n_head
    g_t, g_s = KVT // n_head, KVS // n_head
    n_rank = n_dp * n_kv
    pad = -(-n_s // 8) * 8
    f32, bf16 = jnp.float32, jnp.bfloat16
    dma = pltpu.SemaphoreType.DMA
    kl, loss = pl.pallas_call(
        functools.partial(kernel, n_dp, n_head, n_kv, rows),
        out_shape=(
            jax.ShapeDtypeStruct((1, n_s, rows), f32),
            jax.ShapeDtypeStruct((1, n_s), f32),
        ),
        in_specs=[pl.BlockSpec(memory_space=pltpu.SMEM)]
        + [pl.BlockSpec(memory_space=pl.ANY)] * 4,
        out_specs=(
            pl.BlockSpec(memory_space=pltpu.VMEM),
            pl.BlockSpec(memory_space=pltpu.VMEM),
        ),
        scratch_shapes=[
            pltpu.VMEM((rows, wide_t), bf16),
            pltpu.VMEM((n_kv, rows, g_t * DH), bf16),
            pltpu.VMEM((n_head, rows, n_s * DH), bf16),
            pltpu.VMEM((n_head, n_kv, rows, g_s * DH), bf16),
            pltpu.VMEM((n_t, DH, rows), bf16),
            pltpu.VMEM((HS, DH, rows), bf16),
            pltpu.VMEM((g_t * KVS, 2 * DH + 16, rows), bf16),
            pltpu.VMEM((n_t, 2 * DH + 16, rows), f32),
            pltpu.VMEM((n_t, 1, rows), f32),
            pltpu.VMEM((n_s, 1, rows), f32),
            pltpu.VMEM((n_s, 1, rows), f32),
            pltpu.SMEM((n_t,), jnp.int32),
            pltpu.VMEM((n_head * pad, rows), f32),
            pltpu.VMEM((max(n_head - 1, 1), pad, rows), f32),
            pltpu.VMEM((n_rank, pad, 128), f32),
            dma((4,)),
            dma((3, max(n_head - 1, 1))),
            dma((3, max(n_head - 1, 1))),
            dma((n_kv, n_head + 1)),
            dma((n_kv, n_head + 1)),
            dma((n_rank,)),
            dma((n_rank,)),
        ],
        compiler_params=pltpu.CompilerParams(collective_id=0, has_side_effects=True),
    )(pair_table, teacher_query, teacher_key, student_query, student_key)
    return kl, loss.reshape(n_s)


def solution(mesh):
    split = P("dp", "kv", "head")
    return jax.shard_map(
        per_device,
        mesh=mesh,
        in_specs=(split, split, split, split, P()),
        out_specs=(P("dp", "head", "kv"), P("head")),
        check_vma=False,
    )
```

time: 132 us -> 40.9 us (0.31)
  blocking collectives: 61.4 us -> 0 us
  Pallas kernels: 0 us -> 36.2 us
  waiting for transfers between devices: 33.5 us -> 0 us
  between operations: 16.4 us -> 0.64 us
  local copies, waits for them, and re-layouts: 11.3 us -> 3.8 us
  other arithmetic: 5.49 us -> 0 us
  matrix products: 3.37 us -> 0 us
    psum x1 -> x0, blocking collectives: 39.7 us -> none  [per_device(): total = lax.psum(head_sums, ('dp', 'kv'))]
    pallas_call x0 -> x1, Pallas kernels: none -> 36.2 us  [per_device(): pl.pallas_call(functools.partial(kernel, n_dp, n_head, n_kv, rows), out_s...]
    all_gather x2 -> x0, waiting for transfers between devices: 33.4 us -> none  [the longest x1 26.8 us: per_device(): lax.all_gather(all_tk, 'kv', axis=1, tiled=True)]
    all_gather x2 -> x0, blocking collectives: 21.6 us -> none  [the longest x1 14.4 us: per_device(): lax.all_gather(student_key, 'kv', axis=1, tiled=True)]
    reduce_sum x5 -> x0, other arithmetic: 3.62 us -> none  [the longest x1 2.58 us: one_block(): t_cross = t_cross * t_rescale + jnp.sum(t_weights * gap, axis=-1)]
    dot_general x2 -> x0, matrix products: 3.37 us -> none  [the longest x1 2.58 us: one_block(): jnp.einsum('bqpd,bkpd->bpqk', teacher_heads, t_keys, preferred_element_ty...]
    reshape x5 -> x0, local copies, waits for them, and re-layouts: 3.33 us -> none  [the longest x1 2.89 us: per_device(): all_tq.reshape(seq_dev, row_count, HT, DH)]
    gather x2 -> x0, local copies, waits for them, and re-layouts: 1.62 us -> none  [the longest x1 0.9 us: one_block(): t_keys = jnp.take(t_block, teacher_select, axis=2)]
  transfers between devices with their start and end apart: 2 -> 0, of which waited for: 2 -> 0; matrix products, arithmetic and copies ran while one was open for 5% -> 0% of each run, Pallas kernels for 0% -> 0%
where the time goes in v1:
time: 40.9 us; the launch traced here: 40.6 us
  Pallas kernels  36.2 us (89%)
  local copies, waits for them, and re-layouts  3.8 us (9%)
  between operations  0.64 us (2%)
    pallas_call x1, Pallas kernels, per_device(): pl.pallas_call(functools.partial(kernel, n_dp, n_head, n_kv, rows), out_s...  36.2 us
    unnamed x5, local copies, waits for them, and re-layouts  3.8 us

profile of v1, /device:TPU:0, one launch (start us, length us, event | category | flops | bytes accessed | tf_op | source)
XLA Modules:
  0.0 40.6 jit_solution(12447260519027943394)
XLA Ops:
  0.6 1.4 %copy.7.table = s32[14,2]{1,0:T(8,128)} copy(s32[14,2]{0,1:T(2,128)} %param.9) | data formatting | bytes 224 | tf_op args[4]
  2.0 36.2 %shard_map.68 = (f32[1,7,256]{2,1,0:T(8,128)}, f32[1,7]{1,0:T(1,128)}) custom-call(s32[14,2]{1,0:T(8,128)} %copy.7.table, bf16[1,256,1792]{2,1,0:T(8,128)(2,1)} %tq_hbm.1, bf16[1,256,256]{2,1,0:T(8,128)(2,1)} %tk_hbm.1, bf16[1,256,896]{2,1,0:T(8,128)(2,1)} %sq_hbm.1, bf16[1,256,128]{2,1,0:T(8,128)(2,1)} %sk_hbm.1), custom_call_target="tpu_custom_call" | custom-call | tf_op jit(solution)/shard_map/pallas_call | solution.py:278
  38.2 1.3 %copy.8 = f32[1,7,256]{2,0,1:T(1,128)} copy(f32[1,7,256]{2,1,0:T(8,128)} %get-tuple-element.6) | data formatting | bytes 14336
  39.5 0.0 copy-start
  39.5 0.6 %copy-done = f32[1,7]{1,0:T(1,128)S(1)} copy-done((f32[1,7]{1,0:T(1,128)S(1)}, f32[1,7]{1,0:T(1,128)}, u32[]{:S(2)}) %copy-start) | copy-done | bytes 52
  40.1 0.5 %copy.10 = f32[7]{0:T(128)} copy(f32[7]{0:T(128)S(1)} %bitcast.1) | data formatting | bytes 56
Async XLA Ops:
  39.5 0.6 %copy-start = (f32[1,7]{1,0:T(1,128)S(1)}, f32[1,7]{1,0:T(1,128)}, u32[]{:S(2)}) copy-start(f32[1,7]{1,0:T(1,128)} %get-tuple-element.5) | copy-start | bytes 88

commit v2 on v1

--- a/solution.py
+++ b/solution.py
@@ -37,15 +37,15 @@
     kl_ref, loss_ref,
     tq, tk, sq, sk,
     tq_t, sq_t, key_t, mixed, t_max, s_max, s_sum,
-    inverse, acc, acc_in, sums,
+    inverse, acc, acc_in, sums_out, sums,
     load_sem, x_send, x_recv, z_send, z_recv, sum_send, sum_recv,
 ):
     n_t, n_s = HT // n_head, HS // n_head
     g_t, g_s = KVT // n_head, KVS // n_head
     per_t, per_s = HT // KVT, HS // KVS
     dp, hd, kv = lax.axis_index("dp"), lax.axis_index("head"), lax.axis_index("kv")
-    n_rank = n_dp * n_kv
-    rank = dp * n_kv + kv
+    n_rank = n_dp * n_head * n_kv
+    rank = (dp * n_head + hd) * n_kv + kv
     scale = 1.0 / math.sqrt(DH)
     rate = scale * math.log2(math.e)
 
@@ -60,22 +60,20 @@
 
     barrier = pltpu.get_barrier_semaphore()
 
+    def coordinates(peer):
+        return (peer // (n_head * n_kv), peer // n_kv % n_head, peer % n_kv)
+
     def greet(peer, carry):
         @pl.when(peer != rank)
         def _():
             pl.semaphore_signal(
-                barrier, inc=1, device_id={"dp": peer // n_kv, "kv": peer % n_kv},
-                device_id_type=MESH,
+                barrier, inc=1, device_id=coordinates(peer), device_id_type=MESH
             )
         return carry
 
-    for step in range(1, n_head):
-        pl.semaphore_signal(
-            barrier, inc=1, device_id={"head": (hd + step) % n_head}, device_id_type=MESH
-        )
     lax.fori_loop(0, n_rank, greet, 0)
 
-    entries = [table[k // 2, k % 2] for k in range(HT)]
+    entries = [table[k % 2, k // 2] for k in range(HT)]
     for t in range(n_t):
         found = jnp.int32(0)
         for k in range(HT):
@@ -84,7 +82,7 @@
 
     for load in loads:
         load.wait()
-    pl.semaphore_wait(barrier, n_rank - 1 + n_head - 1)
+    pl.semaphore_wait(barrier, n_rank - 1)
 
     def across(slot, step, src, dst):
         return pltpu.make_async_remote_copy(
@@ -101,6 +99,11 @@
             device_id={"kv": jnp.minimum(kv + 1, n_kv - 1)}, device_id_type=MESH,
         )
 
+    def launch(piece):
+        @pl.when(not_last)
+        def _():
+            upward(kv, piece).start()
+
     pieces = [n_head] + [(hd + s) % n_head for s in range(n_head)]
     not_last = kv < n_kv - 1
 
@@ -109,10 +112,8 @@
     for copy in keys_over:
         copy.start()
 
-    @pl.when(not_last)
-    def _():
-        upward(kv, n_head).start()
-        upward(kv, hd).start()
+    launch(n_head)
+    launch(hd)
 
     for copy in queries_over:
         copy.start()
@@ -126,10 +127,8 @@
     for copy in keys_over:
         copy.wait()
 
-    @pl.when(not_last)
-    def _():
-        for s in range(1, n_head):
-            upward(kv, (hd + s) % n_head).start()
+    for s in range(1, n_head):
+        launch((hd + s) % n_head)
 
     visible = lax.broadcasted_iota(jnp.int32, (rows, rows), 0) <= lax.broadcasted_iota(
         jnp.int32, (rows, rows), 1
@@ -219,18 +218,20 @@
         + [jnp.zeros((1, rows), jnp.float32)] * (pad - n_s),
         axis=0,
     )
-    kl = acc[pl.ds(hd * pad, pad)] + 2.0 * lse
-    for s in range(1, n_head):
-        returns[s - 1].wait()
-        kl = kl + acc_in[s - 1]
-    kl_ref[0] = kl[:n_s]
-    sums[rank] = jnp.broadcast_to(jnp.sum(kl, axis=1, keepdims=True), (pad, 128))
+    mine = jnp.where(place // pad == hd, 2.0 * jnp.concatenate([lse] * n_head, axis=0), 0.0)
+    column = jnp.sum(total + mine, axis=1, keepdims=True)
+    across_lanes = lax.broadcasted_iota(jnp.int32, (n_head * pad, 128), 1)
+    down_rows = lax.broadcasted_iota(jnp.int32, (n_head * pad, 128), 0)
+    for d in range(n_head):
+        sums_out[d] = jnp.sum(
+            jnp.where(down_rows == across_lanes + d * pad, column, 0.0), axis=0, keepdims=True
+        )
 
     def share(peer, place):
         return pltpu.make_async_remote_copy(
-            src_ref=sums.at[rank], dst_ref=sums.at[rank],
+            src_ref=sums_out.at[peer // n_kv % n_head], dst_ref=sums.at[rank],
             send_sem=sum_send.at[peer], recv_sem=sum_recv.at[place],
-            device_id={"dp": peer // n_kv, "kv": peer % n_kv}, device_id_type=MESH,
+            device_id=coordinates(peer), device_id_type=MESH,
         )
 
     def send(peer, carry):
@@ -247,6 +248,13 @@
         return carry
 
     lax.fori_loop(0, n_rank, send, 0)
+    sums[rank] = sums_out[hd]
+    kl = acc[pl.ds(hd * pad, pad)] + 2.0 * lse
+    for s in range(1, n_head):
+        returns[s - 1].wait()
+        kl = kl + acc_in[s - 1]
+    for h in range(n_s):
+        kl_ref[h] = kl[h:h + 1]
 
     @pl.when(not_last)
     def _():
@@ -257,12 +265,13 @@
         lax.fori_loop(0, kv + 1, drain, 0)
 
     lax.fori_loop(0, n_rank, land, 0)
-    whole = jnp.sum(sums[...], axis=0)
-    diagonal = lax.broadcasted_iota(jnp.int32, whole.shape, 0) == lax.broadcasted_iota(
-        jnp.int32, whole.shape, 1
-    )
-    line = jnp.sum(jnp.where(diagonal, whole, 0.0), axis=0, keepdims=True)
+    line = jnp.sum(sums[...], axis=0)
     loss_ref[...] = line[:, :n_s] / (n_dp * rows * n_kv)
+
+
+def finish(kl_in, loss_in, kl_ref, loss_ref):
+    kl_ref[...] = kl_in[...]
+    loss_ref[...] = loss_in[...]
 
 
 def per_device(teacher_query, teacher_key, student_query, student_key, pair_table):
@@ -271,14 +280,14 @@
     assert seq_dev == 1
     n_t, n_s = HT // n_head, HS // n_head
     g_t, g_s = KVT // n_head, KVS // n_head
-    n_rank = n_dp * n_kv
+    n_rank = n_dp * n_head * n_kv
     pad = -(-n_s // 8) * 8
     f32, bf16 = jnp.float32, jnp.bfloat16
     dma = pltpu.SemaphoreType.DMA
     kl, loss = pl.pallas_call(
         functools.partial(kernel, n_dp, n_head, n_kv, rows),
         out_shape=(
-            jax.ShapeDtypeStruct((1, n_s, rows), f32),
+            jax.ShapeDtypeStruct((n_s, 1, rows), f32),
             jax.ShapeDtypeStruct((1, n_s), f32),
         ),
         in_specs=[pl.BlockSpec(memory_space=pltpu.SMEM)]
@@ -302,7 +311,8 @@
             pltpu.SMEM((n_t,), jnp.int32),
             pltpu.VMEM((n_head * pad, rows), f32),
             pltpu.VMEM((max(n_head - 1, 1), pad, rows), f32),
-            pltpu.VMEM((n_rank, pad, 128), f32),
+            pltpu.VMEM((n_head, 1, 128), f32),
+            pltpu.VMEM((n_rank, 1, 128), f32),
             dma((4,)),
             dma((3, max(n_head - 1, 1))),
             dma((3, max(n_head - 1, 1))),
@@ -312,8 +322,20 @@
             dma((n_rank,)),
         ],
         compiler_params=pltpu.CompilerParams(collective_id=0, has_side_effects=True),
-    )(pair_table, teacher_query, teacher_key, student_query, student_key)
-    return kl, loss.reshape(n_s)
+    )(pair_table.T, teacher_query, teacher_key, student_query, student_key)
+    kl, loss = pl.pallas_call(
+        finish,
+        out_shape=(
+            jax.ShapeDtypeStruct((n_s, 1, rows), f32),
+            jax.ShapeDtypeStruct((1, n_s), f32),
+        ),
+        in_specs=[pl.BlockSpec(memory_space=pltpu.VMEM)] * 2,
+        out_specs=(
+            pl.BlockSpec(memory_space=pltpu.VMEM),
+            pl.BlockSpec(memory_space=pltpu.VMEM),
+        ),
+    )(kl, loss)
+    return kl.reshape(1, n_s, rows), loss.reshape(n_s)
 
 
 def solution(mesh):

time: 40.9 us -> 36.6 us (0.89)
  local copies, waits for them, and re-layouts: 3.8 us -> 0 us
    unnamed x5 -> x0, local copies, waits for them, and re-layouts: 3.8 us -> none
    pallas_call x1, Pallas kernels: 36.2 us -> 34.5 us  [per_device(): pl.pallas_call(functools.partial(kernel, n_dp, n_head, n_kv, rows), out_s...]
    pallas_call x0 -> x1, Pallas kernels: none -> 1.3 us  [per_device(): pl.pallas_call(finish, out_shape=(jax.ShapeDtypeStruct((n_s, 1, rows), f3...]
where the time goes in v2:
time: 36.6 us; the launch traced here: 36.4 us
  Pallas kernels  35.8 us (98%)
  between operations  0.64 us (2%)
    pallas_call x1, Pallas kernels, per_device(): pl.pallas_call(functools.partial(kernel, n_dp, n_head, n_kv, rows), out_s...  34.5 us
    pallas_call x1, Pallas kernels, per_device(): pl.pallas_call(finish, out_shape=(jax.ShapeDtypeStruct((n_s, 1, rows), f3...  1.3 us

profile of v2, /device:TPU:0, one launch (start us, length us, event | category | flops | bytes accessed | tf_op | source)
XLA Modules:
  0.0 36.4 jit_solution(5913148939650604362)
XLA Ops:
  0.6 34.5 %shard_map.68 = (f32[7,1,256]{2,1,0:T(1,128)}, f32[1,7]{1,0:T(1,128)}) custom-call(s32[2,14]{1,0:T(2,128)} %bitcast.3, bf16[1,256,1792]{2,1,0:T(8,128)(2,1)} %tq_hbm.1, bf16[1,256,256]{2,1,0:T(8,128)(2,1)} %tk_hbm.1, bf16[1,256,896]{2,1,0:T(8,128)(2,1)} %sq_hbm.1, bf16[1,256,128]{2,1,0:T(8,128)(2,1)} %sk_hbm.1), custom_call_target="tpu_custom_call" | custom-call | tf_op jit(solution)/shard_map/pallas_call | solution.py:287
  35.1 1.3 %shard_map.69 = (f32[7,1,256]{2,1,0:T(1,128)}, f32[1,7]{1,0:T(1,128)}) custom-call(f32[7,1,256]{2,1,0:T(1,128)} %get-tuple-element.6.kl_in, f32[1,7]{1,0:T(1,128)} %get-tuple-element.7.loss_in), custom_call_target="tpu_custom_call" | custom-call | tf_op jit(solution)/shard_map/pallas_call | solution.py:326
